TPU v7x, 32 devices: a whole 2x2x4 slice. The times are simulated.
32 devices in a mesh: dp: 4 (over y, x), mp: 8 (over z, core).
Axes of the slice: x: 2, y: 2, z: 4, core: 2. Of those that a mesh axis runs over, the one named last changes fastest.
Arguments:
- tokens: bfloat16 [128, 6144], P(('dp', 'mp')), may hold values from -6 to 6
- norm_gain: float32 [6144], replicated, may hold values from 0.5 to 1.5
- w_query: bfloat16 [6144, 4096], P('dp', 'mp'), as said below
- w_key: bfloat16 [6144, 4096], P('dp', 'mp'), as said below
- w_value: bfloat16 [6144, 4096], P('dp', 'mp'), may hold values from -0.078125 to 0.078125
- w_inner: bfloat16 [6144, 24576], P('dp', 'mp'), may hold values from -0.078125 to 0.078125
- bias_inner: float32 [24576], P('mp'), may hold values from -3 to 3
- w_attn_out: bfloat16 [4096, 6144], P('mp', 'dp'), may hold values from -0.09375 to 0.09375
- w_outer: bfloat16 [24576, 6144], P('mp', 'dp'), may hold values from -0.0390625 to 0.0390625
- temper: float32 [32], P('mp'), may hold values from 0.5 to 24
Outputs:
- result: bfloat16 [128, 6144], P(('dp', 'mp'))
Inputs may be any that keep to these rules, and one draw needn't show every extreme that they name: `w_query`: entries of order 6144 ** -0.5. `w_key`: entries of order 6144 ** -0.5.
All inputs are finite; a program needn't handle non-finite values.
Results may differ from a plain program's by a relative error of at most 0.023.
Values may be sent and summed in bfloat16 or wider, within the bound.
A program may use at most 128 MiB of HBM per device.

v0:
```python
import math
import jax
import jax.numpy as jnp
from jax import lax
from jax.sharding import PartitionSpec as P

HEAD = 128


def normalize(values):
    center = values - jnp.mean(values, axis=-1, keepdims=True)
    spread = jnp.mean(center * center, axis=-1, keepdims=True)
    return center * lax.rsqrt(spread + 1e-06)


def per_device(
    tokens, norm_gain, w_query, w_key, w_value, w_inner, bias_inner, w_attn_out, w_outer, temper
):
    local = tokens.astype(jnp.float32)
    normed = (normalize(local) * norm_gain).astype(jnp.bfloat16)
    image = lax.all_gather(normed, "mp", axis=0, tiled=True)
    count_rows = image.shape[0]
    width_head = w_query.shape[1]
    spread_rows = lax.all_to_all(image, "dp", split_axis=1, concat_axis=0, tiled=True)
    stacked = jnp.concatenate((w_query, w_key, w_value, w_inner), axis=1)
    projected = lax.psum_scatter(
        jnp.dot(spread_rows, stacked, preferred_element_type=jnp.float32).astype(jnp.bfloat16),
        "dp",
        scatter_dimension=0,
        tiled=True,
    ).astype(jnp.float32)
    query_sum = projected[:, :width_head]
    key_sum = projected[:, width_head : 2 * width_head]
    value_sum = projected[:, 2 * width_head : 3 * width_head]
    inner_sum = projected[:, 3 * width_head :]
    heads_dev = width_head // HEAD
    shape = (count_rows, heads_dev, HEAD)
    query_norm = normalize(
        query_sum.astype(jnp.bfloat16).astype(jnp.float32).reshape(shape)
    ).astype(jnp.bfloat16)
    key_norm = normalize(key_sum.astype(jnp.bfloat16).astype(jnp.float32).reshape(shape)).astype(
        jnp.bfloat16
    )
    values = value_sum.astype(jnp.bfloat16).reshape(shape)
    scale = temper / math.sqrt(HEAD)
    scores = jnp.einsum("qhc,khc->hqk", query_norm, key_norm, preferred_element_type=jnp.float32)
    scores = scores * scale[:, None, None]
    probs = jax.nn.softmax(scores, axis=-1).astype(jnp.bfloat16)
    mixed = jnp.einsum("hqk,khc->qhc", probs, values, preferred_element_type=jnp.float32)
    mixed = mixed.astype(jnp.bfloat16).reshape(count_rows, width_head)
    inner = inner_sum + bias_inner
    activ = jax.nn.gelu(inner, approximate=False).astype(jnp.bfloat16)
    attn_full, outer_full = (
        lax.all_gather(w_attn_out, "dp", axis=1, tiled=True),
        lax.all_gather(w_outer, "dp", axis=1, tiled=True),
    )
    attn_part = lax.psum_scatter(
        jnp.dot(mixed, attn_full, preferred_element_type=jnp.float32).astype(jnp.bfloat16),
        "mp",
        scatter_dimension=0,
        tiled=True,
    ).astype(jnp.float32)
    mlp_part = lax.psum_scatter(
        jnp.dot(activ, outer_full, preferred_element_type=jnp.float32).astype(jnp.bfloat16),
        "mp",
        scatter_dimension=0,
        tiled=True,
    ).astype(jnp.float32)
    total = attn_part + mlp_part
    return (local + total).astype(jnp.bfloat16)


def solution(mesh):
    return jax.shard_map(
        per_device,
        mesh=mesh,
        in_specs=(
            P(("dp", "mp"), None),
            P(),
            P("dp", "mp"),
            P("dp", "mp"),
            P("dp", "mp"),
            P("dp", "mp"),
            P("mp"),
            P("mp", "dp"),
            P("mp", "dp"),
            P("mp"),
        ),
        out_specs=P(("dp", "mp"), None),
        check_vma=False,
    )
```

profile of v0, /device:TPU:0, one launch (start us, length us, event | category | flops | bytes accessed | tf_op | source)
XLA Modules:
  0.0 563.7 jit_solution(12790307825521817195)
XLA Ops:
  6.5 1.0 convert_reduce_fusion
  7.5 1.0 fusion.63
  8.5 0.9 fusion.67
  9.5 16.2 %all-gather = bf16[8,4,6144]{2,1,0:T(4,128)(2,1)S(1)} all-gather(bf16[1,4,6144]{2,1,0:T(4,128)(2,1)S(1)} %fusion.67), channel_id=1, replica_groups=mesh['dp'=4,'mp'=8] {'mp'}, dimensions={0}, use_global_device_ids=true | all-gather | bytes 442368 | tf_op jit(solution)/shard_map/all_gather | solution.py:21
  25.7 0.2 all_to_all.14
  25.9 0.1 copy.32
  26.0 11.1 %all_to_all.19 = bf16[32,4,1536]{2,0,1:T(8,128)(2,1)S(1)} all-to-all(bf16[32,4,1536]{2,0,1:T(8,128)(2,1)S(1)} %copy.32), channel_id=1, replica_groups=mesh['dp'=4,'mp'=8] {'dp'}, dimensions={1} | all-to-all | bytes 786432 | tf_op jit(solution)/shard_map/all_to_all | solution.py:24
  37.2 8.7 %fusion.9 = bf16[128,4608]{1,0:T(8,128)(2,1)} fusion(bf16[128,1536]{1,0:T(8,128)(2,1)S(1)} %bitcast.20, bf16[1536,3072]{1,0:T(8,128)(2,1)} %param.15, bf16[1536,512]{1,0:T(8,128)(2,1)} %param.14, bf16[1536,512]{1,0:T(8,128)(2,1)} %param.13, bf16[1536,512]{1,0:T(8,128)(2,1)} %param.12), kind=kOutput, calls=%fused_computation.11 | convolution fusion | flops 1869152256 | bytes 15728640 | tf_op jit(solution)/shard_map/dot_general | solution.py:27
  45.8 0.0 reduce-scatter.2.cloned.1.call-update
  45.9 0.0 copy-start.1
  45.9 0.0 all-gather.4.cloned.1.call-start
  45.9 0.7 all-gather.4.cloned.1.call-update
  46.6 0.0 all-gather.6.cloned.1.call-start
  46.7 0.7 all-gather.6.cloned.1.call-update
  47.4 0.0 all-reduce.5.cloned.1.call-start
  47.4 26.8 %reduce-scatter.2.cloned.1.call-done = bf16[32,4608]{1,0:T(8,128)(2,1)} async-done(((bf16[128,4608]{1,0:T(8,128)(2,1)}), bf16[32,4608]{1,0:T(8,128)(2,1)}) %reduce-scatter.2.cloned.1.call-update) | async-done | bytes 294928 | tf_op jit(solution)/shard_map/reduce_scatter | solution.py:26
  74.3 0.8 slice_bitcast_fusion
  75.1 0.1 reduce_sum.65
  75.2 0.1 reduce_sum.67
  75.4 0.2 multiply_reduce_fusion.1
  75.6 0.2 multiply_reduce_fusion
  75.8 0.2 multiply_convert_fusion
  76.0 0.2 fusion.110
  76.2 0.2 fusion.14
  76.4 69.8 %all-gather.4.cloned.1.call-done = bf16[512,6144]{1,0:T(8,128)(2,1)} async-done(((bf16[512,1536]{1,0:T(8,128)(2,1)}), bf16[512,6144]{1,0:T(8,128)(2,1)}) %all-gather.4.cloned.1.call-update) | async-done | bytes 6291472 | tf_op jit(solution)/shard_map/all_gather | solution.py:54
  146.2 4.7 convolution_convert_fusion.1
  150.9 330.0 %all-gather.6.cloned.1.call-done = bf16[3072,6144]{1,0:T(8,128)(2,1)} async-done(((bf16[3072,1536]{1,0:T(8,128)(2,1)}), bf16[3072,6144]{1,0:T(8,128)(2,1)}) %all-gather.6.cloned.1.call-update) | async-done | bytes 37748752 | tf_op jit(solution)/shard_map/all_gather | solution.py:55
  480.9 16.6 %convolution_convert_fusion = bf16[32,6144]{1,0:T(8,128)(2,1)} fusion(bf16[3072,6144]{1,0:T(8,128)(2,1)} %all-gather.6.cloned.1.call-done, bf16[32,4608]{1,0:T(8,128)(2,1)} %reduce-scatter.2.cloned.1.call-done, f32[3072]{0:T(1024)S(1)} %copy-done.1), kind=kOutput, calls=%fused_computation.9 | convolution fusion | flops 1214742528 | bytes 38350848 | tf_op jit(solution)/shard_map/dot_general | solution.py:64
  497.5 0.0 all-reduce.5.cloned.1.call-update
  497.5 0.6 dynamic-slice
  498.8 56.7 %all-reduce.5.cloned.1.call-done = (bf16[32,6144]{1,0:T(8,128)(2,1)}, bf16[32,6144]{1,0:T(8,128)(2,1)}) async-done(((bf16[32,6144]{1,0:T(8,128)(2,1)}, bf16[32,6144]{1,0:T(8,128)(2,1)}), (bf16[32,6144]{1,0:T(8,128)(2,1)}, bf16[32,6144]{1,0:T(8,128)(2,1)})) %all-reduce.5.cloned.1.call-update) | async-done | bytes 786448
  555.5 1.6 fusion.66
  (17 shorter events, 0.1 us)
Async XLA Ops:
  6.5 67.7 %reduce-scatter.2.cloned.1.call-start = ((), (), s32[]{:S(2)}) async-start(), calls=%async_computation.2 | async-start | bytes 1474560 | tf_op jit(solution)/shard_map/reduce_scatter | solution.py:26
  45.8 1.6 copy-start.2
  45.9 435.1 %copy-start.1 = (f32[3072]{0:T(1024)S(1)}, f32[3072]{0:T(1024)}, u32[]{:S(2)}) copy-start(f32[3072]{0:T(1024)} %param.16) | copy-start | bytes 36868
  45.9 100.3 %all-gather.4.cloned.1.call-start = ((), (), s32[]{:S(2)}) async-start(), calls=%async_computation.3 | async-start | bytes 7864320 | tf_op jit(solution)/shard_map/all_gather | solution.py:54
  46.6 434.3 %all-gather.6.cloned.1.call-start = ((), (), s32[]{:S(2)}) async-start(), calls=%async_computation.4 | async-start | bytes 47185920 | tf_op jit(solution)/shard_map/all_gather | solution.py:55
  47.4 508.1 %all-reduce.5.cloned.1.call-start = ((), (), s32[]{:S(2)}) async-start(), calls=%async_computation.5 | async-start | bytes 1572864
  150.9 346.6 %copy-start.3 = (u32[32]{0:T(128)S(1)}, u32[32]{0:T(128)}, u32[]{:S(2)}) copy-start(u32[32]{0:T(128)} %constant.84) | copy-start | bytes 388
  150.9 404.6 %copy-start = (bf16[4,6144]{1,0:T(4,128)(2,1)S(1)}, bf16[4,6144]{1,0:T(4,128)(2,1)}, u32[]{:S(2)}) copy-start(bf16[4,6144]{1,0:T(4,128)(2,1)} %param.10) | copy-start | bytes 147460
Sparse Core Ops, SparseCore 0:
  46.0 28.2 reduce-scatter.1
  76.1 70.0 all-gather.3
  148.0 332.8 all-gather.5
  497.6 57.8 all-reduce.4
where the time goes:
time: 564 us
  waiting for transfers between devices  485 us (86%)
  matrix products  30.4 us (5%)
  blocking collectives  27.4 us (5%)
  between operations  13.9 us (2%)
  other arithmetic  6.14 us (1%)
    all_gather x1, waiting for transfers between devices, per_device(): lax.all_gather(w_outer, 'dp', axis=1, tiled=True)  330 us
    all_gather x1, waiting for transfers between devices, per_device(): lax.all_gather(w_attn_out, 'dp', axis=1, tiled=True)  69.8 us
    unnamed x5, waiting for transfers between devices  58.1 us
    reduce_scatter x1, waiting for transfers between devices, per_device(): lax.psum_scatter(jnp.dot(spread_rows, stacked, preferred_element_type=jnp...  26.8 us
    dot_general x1, matrix products, per_device(): jnp.dot(activ, outer_full, preferred_element_type=jnp.float32)  16.6 us
    all_gather x1, blocking collectives, per_device(): image = lax.all_gather(normed, 'mp', axis=0, tiled=True)  16.2 us
  transfers between devices with their start and end apart: 4, of which 4 were waited for; matrix products, arithmetic and copies ran while one was open for 1% of the time, Pallas kernels for 0%

commit v1 on v0

--- a/solution.py
+++ b/solution.py
@@ -5,6 +5,13 @@
 from jax.sharding import PartitionSpec as P
 
 HEAD = 128
+
+
+def exchange_gather(array, name, dim):
+    peers = lax.axis_size(name)
+    blocks = jnp.stack([array for _ in range(peers)])
+    blocks = lax.all_to_all(blocks, name, split_axis=0, concat_axis=0)
+    return jnp.concatenate(blocks, axis=dim)
 
 
 def normalize(values):
@@ -51,7 +58,7 @@
     inner = inner_sum + bias_inner
     activ = jax.nn.gelu(inner, approximate=False).astype(jnp.bfloat16)
     attn_full, outer_full = (
-        lax.all_gather(w_attn_out, "dp", axis=1, tiled=True),
+        exchange_gather(w_attn_out, "dp", 1),
         lax.all_gather(w_outer, "dp", axis=1, tiled=True),
     )
     attn_part = lax.psum_scatter(

time: 564 us -> 551 us (0.977)
  waiting for transfers between devices: 485 us -> 461 us
    all_gather x1 -> x0, waiting for transfers between devices: 69.8 us -> none  [per_device(): lax.all_gather(w_attn_out, 'dp', axis=1, tiled=True)]
    reduce_scatter x1, waiting for transfers between devices: 26.8 us -> 56.4 us  [per_device(): lax.psum_scatter(jnp.dot(spread_rows, stacked, preferred_element_type=jnp...]
    all_to_all x0 -> x1, waiting for transfers between devices: none -> 16.5 us  [exchange_gather(): blocks = lax.all_to_all(blocks, name, split_axis=0, concat_axis=0)]
    unnamed x5 -> x4, waiting for transfers between devices: 58.1 us -> 57.5 us
  transfers between devices with their start and end apart: 4 -> 4, of which waited for: 4 -> 4; matrix products, arithmetic and copies ran while one was open for 1% -> 2% of each run, Pallas kernels for 0% -> 0%
where the time goes in v1:
time: 551 us; the launch traced here: 550 us
  waiting for transfers between devices  461 us (84%)
  matrix products  31.1 us (6%)
  blocking collectives  27.4 us (5%)
  between operations  13.9 us (3%)
  other arithmetic  6.14 us (1%)
    all_gather x1, waiting for transfers between devices, per_device(): lax.all_gather(w_outer, 'dp', axis=1, tiled=True)  330 us
    unnamed x4, waiting for transfers between devices  57.5 us
    reduce_scatter x1, waiting for transfers between devices, per_device(): lax.psum_scatter(jnp.dot(spread_rows, stacked, preferred_element_type=jnp...  56.4 us
    dot_general x1, matrix products, per_device(): jnp.dot(activ, outer_full, preferred_element_type=jnp.float32)  16.6 us
    all_to_all x1, waiting for transfers between devices, exchange_gather(): blocks = lax.all_to_all(blocks, name, split_axis=0, concat_axis=0)  16.5 us
    all_gather x1, blocking collectives, per_device(): image = lax.all_gather(normed, 'mp', axis=0, tiled=True)  16.2 us
    all_to_all x1, blocking collectives, per_device(): lax.all_to_all(image, 'dp', split_axis=1, concat_axis=0, tiled=True)  11.1 us
  transfers between devices with their start and end apart: 4, of which 4 were waited for; matrix products, arithmetic and copies ran while one was open for 2% of the time, Pallas kernels for 0%

profile of v1, /device:TPU:0, one launch (start us, length us, event | category | flops | bytes accessed | tf_op | source)
XLA Modules:
  0.0 550.1 jit_solution(17703773488470072747)
XLA Ops:
  6.5 1.0 convert_reduce_fusion
  7.5 1.0 fusion.63
  8.5 0.9 fusion.67
  9.5 16.2 %all-gather = bf16[8,4,6144]{2,1,0:T(4,128)(2,1)S(1)} all-gather(bf16[1,4,6144]{2,1,0:T(4,128)(2,1)S(1)} %fusion.67), channel_id=1, replica_groups=mesh['dp'=4,'mp'=8] {'mp'}, dimensions={0}, use_global_device_ids=true | all-gather | bytes 442368 | tf_op jit(solution)/shard_map/all_gather | solution.py:28
  25.7 0.2 all_to_all.17
  25.9 0.1 copy.35
  26.0 11.1 %all_to_all.24 = bf16[32,4,1536]{2,0,1:T(8,128)(2,1)S(1)} all-to-all(bf16[32,4,1536]{2,0,1:T(8,128)(2,1)S(1)} %copy.35), channel_id=1, replica_groups=mesh['dp'=4,'mp'=8] {'dp'}, dimensions={1} | all-to-all | bytes 786432 | tf_op jit(solution)/shard_map/all_to_all | solution.py:31
  37.2 8.7 %fusion.9 = bf16[128,4608]{1,0:T(8,128)(2,1)} fusion(bf16[128,1536]{1,0:T(8,128)(2,1)S(1)} %bitcast.23, bf16[1536,3072]{1,0:T(8,128)(2,1)} %param.15, bf16[1536,512]{1,0:T(8,128)(2,1)} %param.14, bf16[1536,512]{1,0:T(8,128)(2,1)} %param.13, bf16[1536,512]{1,0:T(8,128)(2,1)} %param.12), kind=kOutput, calls=%fused_computation.11 | convolution fusion | flops 1869152256 | bytes 15728640 | tf_op jit(solution)/shard_map/dot_general | solution.py:34
  45.8 0.0 reduce-scatter.2.cloned.1.call-update
  45.9 0.0 all-gather.3.cloned.1.call-start
  45.9 0.7 all-gather.3.cloned.1.call-update
  46.6 0.6 copy-done
  47.3 0.7 copy.41
  48.0 3.1 stack.2
  51.0 5.4 all-to-all-start.1
  56.4 0.0 all-reduce.5.cloned.1.call-start
  56.5 56.4 %reduce-scatter.2.cloned.1.call-done = bf16[32,4608]{1,0:T(8,128)(2,1)} async-done(((bf16[128,4608]{1,0:T(8,128)(2,1)}), bf16[32,4608]{1,0:T(8,128)(2,1)}) %reduce-scatter.2.cloned.1.call-update) | async-done | bytes 294928 | tf_op jit(solution)/shard_map/reduce_scatter | solution.py:33
  112.9 0.8 slice_bitcast_fusion
  113.8 0.1 reduce_sum.67
  113.9 0.1 reduce_sum.65
  114.0 0.2 multiply_reduce_fusion
  114.2 0.2 multiply_reduce_fusion.1
  114.4 0.2 multiply_convert_fusion
  114.7 0.2 fusion.110
  114.8 0.2 fusion.14
  115.0 16.5 %all-to-all-done.1 = bf16[4,512,1536]{1,2,0:T(8,128)(2,1)} async-done(((bf16[4,512,1536]{1,2,0:T(8,128)(2,1)}), bf16[4,512,1536]{1,2,0:T(8,128)(2,1)}, u32[]{:S(2)}, u32[]{:S(2)}) %all-to-all-start.1) | async-done | bytes 6291488 | tf_op jit(solution)/shard_map/all_to_all | solution.py:13
  131.5 5.5 convolution_convert_fusion.1
  137.0 330.4 %all-gather.3.cloned.1.call-done = bf16[3072,6144]{1,0:T(8,128)(2,1)} async-done(((bf16[3072,1536]{1,0:T(8,128)(2,1)}), bf16[3072,6144]{1,0:T(8,128)(2,1)}) %all-gather.3.cloned.1.call-update) | async-done | bytes 37748752 | tf_op jit(solution)/shard_map/all_gather | solution.py:62
  467.4 16.6 %convolution_convert_fusion = bf16[32,6144]{1,0:T(8,128)(2,1)} fusion(bf16[3072,6144]{1,0:T(8,128)(2,1)} %all-gather.3.cloned.1.call-done, bf16[32,4608]{1,0:T(8,128)(2,1)} %reduce-scatter.2.cloned.1.call-done, f32[3072]{0:T(1024)S(1)} %copy-done.2), kind=kOutput, calls=%fused_computation.9 | convolution fusion | flops 1214742528 | bytes 38350848 | tf_op jit(solution)/shard_map/dot_general | solution.py:71
  484.0 0.6 dynamic-slice
  485.2 56.7 %all-reduce.5.cloned.1.call-done = (bf16[32,6144]{1,0:T(8,128)(2,1)}, bf16[32,6144]{1,0:T(8,128)(2,1)}) async-done(((bf16[32,6144]{1,0:T(8,128)(2,1)}, bf16[32,6144]{1,0:T(8,128)(2,1)}), (bf16[32,6144]{1,0:T(8,128)(2,1)}, bf16[32,6144]{1,0:T(8,128)(2,1)})) %all-reduce.5.cloned.1.call-update) | async-done | bytes 786448
  542.0 1.6 fusion.66
  (20 shorter events, 0.1 us)
Async XLA Ops:
  6.5 106.4 %reduce-scatter.2.cloned.1.call-start = ((), (), s32[]{:S(2)}) async-start(), calls=%async_computation.3 | async-start | bytes 1474560 | tf_op jit(solution)/shard_map/reduce_scatter | solution.py:33
  45.8 1.4 copy-start
  45.9 421.5 %all-gather.3.cloned.1.call-start = ((), (), s32[]{:S(2)}) async-start(), calls=%async_computation.4 | async-start | bytes 47185920 | tf_op jit(solution)/shard_map/all_gather | solution.py:62
  48.0 8.5 %copy-start.3 = (f32[4]{0:T(128)S(1)}, f32[4]{0:T(128)}, u32[]{:S(2)}) copy-start(f32[4]{0:T(128)} %param.19) | copy-start | bytes 52
  51.0 416.4 %copy-start.2 = (f32[3072]{0:T(1024)S(1)}, f32[3072]{0:T(1024)}, u32[]{:S(2)}) copy-start(f32[3072]{0:T(1024)} %param.16) | copy-start | bytes 36868
  51.0 80.5 %all-to-all-start.1 = ((bf16[4,512,1536]{1,2,0:T(8,128)(2,1)}), bf16[4,512,1536]{1,2,0:T(8,128)(2,1)}, u32[]{:S(2)}, u32[]{:S(2)}) async-start(bf16[4,512,1536]{1,2,0:T(8,128)(2,1)} %stack.2), calls=%async_computation.2 | async-start | bytes 12582912 | tf_op jit(solution)/shard_map/all_to_all | solution.py:13
  56.4 485.6 %all-reduce.5.cloned.1.call-start = ((), (), s32[]{:S(2)}) async-start(), calls=%async_computation.5 | async-start | bytes 1572864
  137.0 347.0 %copy-start.4 = (u32[32]{0:T(128)S(1)}, u32[32]{0:T(128)}, u32[]{:S(2)}) copy-start(u32[32]{0:T(128)} %constant.84) | copy-start | bytes 388
  137.0 405.0 %copy-start.1 = (bf16[4,6144]{1,0:T(4,128)(2,1)S(1)}, bf16[4,6144]{1,0:T(4,128)(2,1)}, u32[]{:S(2)}) copy-start(bf16[4,6144]{1,0:T(4,128)(2,1)} %param.10) | copy-start | bytes 147460
Sparse Core Ops, SparseCore 0:
  46.0 66.8 reduce-scatter.1
  114.8 352.5 all-gather.2
  484.1 57.8 all-reduce.4
